TPU v7x, 32 devices: a whole 2x2x4 slice. The times are simulated.
32 devices in a mesh: group: 2 (over y), fsdp: 16 (over z, x, core).
Axes of the slice: x: 2, y: 2, z: 4, core: 2. Of those that a mesh axis runs over, the one named last changes fastest.
Arguments:
- acts: bfloat16 [2, 8192, 8192], P('group', 'fsdp'), may hold values from -6 to 6
- cotangent: bfloat16 [2, 8192, 512], P('group', 'fsdp'), may hold values from -5.40625 to 5.40625
- inner_params: float32 [2, 8192, 512], P('group', 'fsdp'), may hold values from -6 to 6
- adam_first: float32 [2, 8192, 512], P('group', 'fsdp'), may hold values from -0.018 to 0.018
- adam_second: float32 [2, 8192, 512], P('group', 'fsdp'), may hold values from 1e-06 to 0.0001
- inner_steps: int32 [2], replicated, may hold values from 8 to 128
- group_tokens: int32 [2], replicated, may hold values from 16384 to 131072
- anchor: float32 [8192, 512], P(('fsdp', 'group')), may hold values from -6 to 6
- momentum: float32 [8192, 512], P(('fsdp', 'group')), may hold values from -2 to 2
Outputs:
- new_anchor: float32 [8192, 512], P(('fsdp', 'group'))
- new_momentum: float32 [8192, 512], P(('fsdp', 'group'))
- group_weights: bfloat16 [2, 8192, 512], P('group', 'fsdp')
All inputs are finite; a program needn't handle non-finite values.
Results may differ from a plain program's by a relative error of at most 0.0004.
Values may be sent and summed in bfloat16 or wider, within the bound.
A program may use at most 128 MiB of HBM per device.

v0:
```python
import jax
import jax.numpy as jnp
from jax import lax
from jax.sharding import PartitionSpec as P

beta_one = 0.9
beta_two = 0.95
epsilon = 1e-08
inner_rate = 0.3
decay_rate = 0.1
outer_rate = 0.7
outer_mom = 0.9


def inner_update(params, first_moment, second_moment, gradient, steps):
    fresh_first = beta_one * first_moment + (1.0 - beta_one) * gradient
    fresh_second = beta_two * second_moment + (1.0 - beta_two) * gradient * gradient
    steps_float = steps.astype(jnp.float32)
    correct_one = 1.0 - jnp.power(jnp.float32(beta_one), steps_float)
    correct_two = 1.0 - jnp.power(jnp.float32(beta_two), steps_float)
    ratio = fresh_first / correct_one / (jnp.sqrt(fresh_second / correct_two) + epsilon)
    return params - inner_rate * (ratio + decay_rate * params)


def outer_update(anchor, momentum, merged):
    pseudo = anchor - merged
    fresh_momentum = outer_mom * momentum + pseudo
    fresh_anchor = anchor - outer_rate * (pseudo + outer_mom * fresh_momentum)
    return (fresh_anchor, fresh_momentum)


def per_device(
    acts,
    cotangent,
    inner_params,
    adam_first,
    adam_second,
    inner_steps,
    group_tokens,
    anchor,
    momentum,
):
    fsdp_count = lax.axis_size("fsdp")
    group_index = lax.axis_index("group")
    inputs = acts[0]
    upstream = cotangent[0]
    group_total = inputs.shape[0] * fsdp_count
    contract = (((0,), (0,)), ((), ()))
    summed = lax.psum_scatter(
        lax.dot_general(inputs, upstream, contract, preferred_element_type=jnp.float32),
        "fsdp",
        scatter_dimension=0,
        tiled=True,
    )
    gradient = summed / group_total
    steps = lax.dynamic_index_in_dim(inner_steps, group_index, 0, False)
    updated = inner_update(inner_params[0], adam_first[0], adam_second[0], gradient, steps)
    counts = group_tokens.astype(jnp.float32)
    share = lax.dynamic_index_in_dim(counts, group_index, 0, False) / jnp.sum(counts)
    weighted = share * updated
    merged = lax.psum_scatter(weighted, "group", scatter_dimension=0, tiled=True)
    new_anchor, new_momentum = outer_update(anchor, momentum, merged)
    rebuilt = lax.all_gather(new_anchor.astype(jnp.bfloat16), "group", axis=0, tiled=True)
    return (new_anchor, new_momentum, rebuilt[None])


def solution(mesh):
    placed = (
        P("group", "fsdp", None),
        P("group", "fsdp", None),
        P("group", "fsdp", None),
        P("group", "fsdp", None),
        P("group", "fsdp", None),
        P(),
        P(),
        P(("fsdp", "group"), None),
        P(("fsdp", "group"), None),
    )
    return jax.shard_map(
        per_device,
        mesh=mesh,
        in_specs=placed,
        out_specs=(
            P(("fsdp", "group"), None),
            P(("fsdp", "group"), None),
            P("group", "fsdp", None),
        ),
        check_vma=False,
    )
```

profile of v0, /device:TPU:0, one launch (start us, length us, event | category | flops | bytes accessed | tf_op | source)
XLA Modules:
  0.0 241.7 jit_solution(1804478649830229206)
XLA Ops:
  7.2 0.0 copy-start
  7.2 0.0 reduce-scatter.3.cloned.1.call-start
  7.2 1.0 copy-done
  8.2 11.7 %fusion = f32[8192,512]{1,0:T(8,128)} fusion(bf16[1,512,8192]{2,1,0:T(8,128)(2,1)} %param.9, bf16[1,512,512]{2,1,0:T(8,128)(2,1)S(1)} %copy-done), kind=kOutput, calls=%fused_computation | convolution fusion | flops 4294967296 | bytes 25690112 | tf_op jit(solution)/shard_map/dot_general | solution.py:50
  19.9 0.0 copy-start.4
  19.9 0.0 copy-start.5
  19.9 0.0 copy-start.1
  19.9 0.0 copy-start.2
  19.9 0.0 copy-start.3
  19.9 0.0 reduce-scatter.3.cloned.1.call-update
  19.9 0.0 reduce-scatter.5.cloned.1.call-start
  20.0 0.6 copy-done.4
  20.5 0.6 dynamic_slice.9
  21.8 0.0 copy-done.5
  21.9 0.6 dynamic_slice.8
  22.5 0.6 convert_reduce_fusion
  24.3 175.8 %reduce-scatter.3.cloned.1.call-done = f32[512,512]{1,0:T(8,128)} async-done(((f32[8192,512]{1,0:T(8,128)}), f32[512,512]{1,0:T(8,128)}) %reduce-scatter.3.cloned.1.call-update) | async-done | bytes 1048592 | tf_op jit(solution)/shard_map/reduce_scatter | solution.py:49
  200.1 0.0 copy-done.1
  200.1 0.0 copy-done.2
  200.1 3.4 %fusion.8 = f32[512,512]{1,0:T(8,128)} fusion(f32[1,512,512]{2,1,0:T(8,128)S(1)} %copy-done.1, f32[512,512]{1,0:T(8,128)} %reduce-scatter.3.cloned.1.call-done, f32[1,512,512]{2,1,0:T(8,128)S(1)} %copy-done.2, f32[1,512,512]{2,1,0:T(8,128)} %param.12, f32[]{:T(128)} %bitcast.7, f32[]{:T(128)} %bitcast.5, f32[]{:T(128)S(6)} %div.22), kind=kLoop, calls=%fused_computation.12 | loop fusion | flops 4456448 | bytes 5242892 | tf_op jit(solution)/shard_map/mul | solution.py:60
  203.5 0.0 reduce-scatter.5.cloned.1.call-update
  203.5 19.7 %reduce-scatter.5.cloned.1.call-done = f32[256,512]{1,0:T(8,128)} async-done(((f32[512,512]{1,0:T(8,128)}), f32[256,512]{1,0:T(8,128)}) %reduce-scatter.5.cloned.1.call-update) | async-done | bytes 524304 | tf_op jit(solution)/shard_map/reduce_scatter | solution.py:61
  223.2 0.0 copy-done.3
  223.2 2.4 fusion.10
  225.6 8.5 %all_gather.3 = bf16[512,512]{1,0:T(8,128)(2,1)S(1)} all-gather(bf16[256,512]{1,0:T(8,128)(2,1)S(1)} %get-tuple-element.3), channel_id=1, replica_groups=mesh['group'=2,'fsdp'=16] {'group'}, dimensions={0}, use_global_device_ids=true | all-gather | bytes 786432 | tf_op jit(solution)/shard_map/all_gather | solution.py:63
  234.1 0.8 copy.13
  (1 shorter events, 0.0 us)
Async XLA Ops:
  7.2 1.0 copy-start
  7.2 193.0 %reduce-scatter.3.cloned.1.call-start = ((), (), s32[]{:S(2)}) async-start(), calls=%async_computation.2 | async-start | bytes 17825792 | tf_op jit(solution)/shard_map/reduce_scatter | solution.py:49
  19.9 0.7 copy-start.4
  19.9 2.0 copy-start.5
  19.9 180.3 %copy-start.1 = (f32[1,512,512]{2,1,0:T(8,128)S(1)}, f32[1,512,512]{2,1,0:T(8,128)}, u32[]{:S(2)}) copy-start(f32[1,512,512]{2,1,0:T(8,128)} %param.11) | copy-start | bytes 3145732
  19.9 180.3 %copy-start.2 = (f32[1,512,512]{2,1,0:T(8,128)S(1)}, f32[1,512,512]{2,1,0:T(8,128)}, u32[]{:S(2)}) copy-start(f32[1,512,512]{2,1,0:T(8,128)} %param.13) | copy-start | bytes 3145732
  19.9 203.3 %copy-start.3 = (f32[256,512]{1,0:T(8,128)S(1)}, f32[256,512]{1,0:T(8,128)}, u32[]{:S(2)}) copy-start(f32[256,512]{1,0:T(8,128)} %param.16) | copy-start | bytes 1572868
  19.9 203.3 %reduce-scatter.5.cloned.1.call-start = ((), (), s32[]{:S(2)}) async-start(), calls=%async_computation.3 | async-start | bytes 1572864 | tf_op jit(solution)/shard_map/reduce_scatter | solution.py:61
Sparse Core Ops, SparseCore 0:
  20.0 180.0 reduce-scatter.2
  203.7 19.4 reduce-scatter.4
where the time goes:
time: 242 us
  waiting for transfers between devices  196 us (81%)
  between operations  16.1 us (7%)
  matrix products  11.7 us (5%)
  blocking collectives  8.52 us (4%)
  other arithmetic  6.32 us (3%)
  local copies, waits for them, and re-layouts  3.53 us (1%)
    reduce_scatter x1, waiting for transfers between devices, per_device(): lax.psum_scatter(lax.dot_general(inputs, upstream, contract, preferred_el...  176 us
    reduce_scatter x1, waiting for transfers between devices, per_device(): lax.psum_scatter(weighted, 'group', scatter_dimension=0, tiled=True)  19.7 us
    dot_general x1, matrix products, per_device(): lax.dot_general(inputs, upstream, contract, preferred_element_type=jnp.fl...  11.7 us
    all_gather x1, blocking collectives, per_device(): lax.all_gather(new_anchor.astype(jnp.bfloat16), 'group', axis=0, tiled=True)  8.52 us
  transfers between devices with their start and end apart: 2, of which 2 were waited for; matrix products, arithmetic and copies ran while one was open for 1% of the time, Pallas kernels for 0%

commit v1 on v0

--- a/solution.py
+++ b/solution.py
@@ -1,6 +1,10 @@
+import functools
+
 import jax
 import jax.numpy as jnp
 from jax import lax
+from jax.experimental import pallas as pl
+from jax.experimental.pallas import tpu as pltpu
 from jax.sharding import PartitionSpec as P
 
 beta_one = 0.9
@@ -64,6 +68,368 @@
     return (new_anchor, new_momentum, rebuilt[None])
 
 
+MESH = pl.DeviceIdType.MESH
+WIRE = jnp.int16
+LEVELS = 32767.0
+SMALLEST = 1e-30
+PIECES = 4
+HALVES = 2
+FIRST_ORDER = (1, 2, 3)
+OTHER_ORDER = (2, 1, 3)
+ORDERS = (FIRST_ORDER, OTHER_ORDER, FIRST_ORDER, FIRST_ORDER)
+STEPS = 3
+PLAN = (
+    ("mul", 0, 1), ("mul", 1, 1), ("mul", 2, 1), ("mul", 0, 0), ("mul", 1, 0),
+    ("add", 0, 0, 1), ("add", 1, 0, 1), ("add", 0, 1, 1), ("add", 1, 1, 1),
+    ("mul", 3, 1), ("mul", 2, 0), ("mul", 3, 0),
+    ("add", 0, 0, 2), ("add", 0, 1, 2), ("add", 2, 0, 1), ("add", 0, 0, 3),
+    ("add", 2, 0, 2), ("add", 2, 1, 1), ("add", 0, 1, 3), ("add", 1, 0, 2),
+    ("add", 2, 1, 2), ("add", 2, 0, 3), ("add", 1, 1, 2), ("add", 1, 0, 3),
+    ("add", 2, 1, 3), ("add", 1, 1, 3), ("add", 3, 0, 1), ("add", 3, 0, 2),
+    ("add", 3, 1, 1), ("add", 3, 0, 3), ("add", 3, 1, 2), ("add", 3, 1, 3),
+)
+
+
+def outer_step_kernel(
+    group_total,
+    scalars,
+    acts,
+    cotangent,
+    params_in,
+    first_in,
+    second_in,
+    anchor_in,
+    momentum_in,
+    anchor_out,
+    momentum_out,
+    weights_out,
+    acts_buf,
+    cot_buf,
+    cot_t,
+    own,
+    send1,
+    send2,
+    send3,
+    recv1,
+    recv2,
+    recv3,
+    scale_send,
+    scale_recv,
+    params,
+    first,
+    second,
+    anchor,
+    momentum,
+    weighted_send,
+    weighted_recv,
+    fresh_send,
+    fresh_recv,
+    local_sem,
+    acts_send_sem,
+    acts_recv_sem,
+    cot_sem,
+    state_sem,
+    step_send_sem,
+    step_recv_sem,
+    scale_send_sem,
+    scale_recv_sem,
+    weighted_send_sem,
+    weighted_recv_sem,
+    fresh_send_sem,
+    fresh_recv_sem,
+):
+    tokens, _ = acts.shape
+    rows, width = params.shape
+    cols = rows // PIECES
+    half_width = width // HALVES
+    half_rows = rows // 2
+    me = lax.axis_index("fsdp")
+    group = lax.axis_index("group")
+    other_group = 1 - group
+    bits = [(me // (1 << k)) % 2 for k in range(STEPS + 1)]
+
+    def across(k):
+        return (group, me + (1 - 2 * bits[k]) * (1 << k))
+
+    sibling = across(0)
+    peer = (other_group, me)
+    sends, recvs = (send1, send2, send3), (recv1, recv2, recv3)
+
+    state = []
+    for n, (src, dst) in enumerate(
+        ((params_in, params), (first_in, first), (second_in, second), (anchor_in, anchor), (momentum_in, momentum))
+    ):
+        state.append(pltpu.make_async_copy(src, dst, state_sem.at[n]))
+    cot_local = pltpu.make_async_copy(cotangent, cot_buf.at[pl.ds(0, tokens)], cot_sem.at[0])
+    cot_remote = pltpu.make_async_remote_copy(
+        src_ref=cotangent,
+        dst_ref=cot_buf.at[pl.ds(tokens, tokens)],
+        send_sem=cot_sem.at[1],
+        recv_sem=cot_sem.at[2],
+        device_id=sibling,
+        device_id_type=MESH,
+    )
+
+    def column_piece(i):
+        return (other_group * (PIECES // 2) + i) % PIECES
+
+    def acts_columns(i, pos, core):
+        block = core
+        for s, k in enumerate(ORDERS[i]):
+            bit = bits[k] if (pos >> (STEPS - 1 - s)) % 2 == 0 else 1 - bits[k]
+            block = block + bit * (1 << k)
+        return pl.ds(pl.multiple_of(block * rows + column_piece(i) * cols, cols), cols)
+
+    acts_remote = {}
+    acts_local = {}
+    for i in range(PIECES):
+        for pos in range(8):
+            acts_local[i, pos] = pltpu.make_async_copy(
+                acts.at[:, acts_columns(i, pos, bits[0])],
+                acts_buf.at[i, pos, pl.ds(0, tokens)],
+                local_sem.at[i, pos],
+            )
+            acts_remote[i, pos] = pltpu.make_async_remote_copy(
+                src_ref=acts.at[:, acts_columns(i, pos, 1 - bits[0])],
+                dst_ref=acts_buf.at[i, pos, pl.ds(tokens, tokens)],
+                send_sem=acts_send_sem.at[i, pos],
+                recv_sem=acts_recv_sem.at[i, pos],
+                device_id=sibling,
+                device_id_type=MESH,
+            )
+
+    barrier = pltpu.get_barrier_semaphore()
+    for target in (sibling, across(1), across(2), across(3), peer):
+        pl.semaphore_signal(barrier, inc=1, device_id=target, device_id_type=MESH)
+    cot_local.start()
+    need = [(e[1], e[2]) for e in PLAN if e[0] == "mul"]
+    for i, part in need:
+        for pos in range(4 * part, 4 * part + 4):
+            acts_local[i, pos].start()
+    for copy in state:
+        copy.start()
+    pl.semaphore_wait(barrier, 5)
+    cot_remote.start()
+    for i, part in need:
+        for pos in range(4 * part, 4 * part + 4):
+            acts_remote[i, pos].start()
+
+    scale_send[...] = jnp.zeros_like(scale_send)
+    cot_local.wait()
+    cot_remote.wait_recv()
+    cot_t[...] = cot_buf[...].astype(jnp.float32).T.astype(jnp.bfloat16)
+
+    flying = []
+
+    def send_step(i, h, step):
+        copy = pltpu.make_async_remote_copy(
+            src_ref=sends[step - 1].at[i, h],
+            dst_ref=recvs[step - 1].at[i, h],
+            send_sem=step_send_sem.at[step - 1, i, h],
+            recv_sem=step_recv_sem.at[step - 1, i, h],
+            device_id=across(ORDERS[i][step - 1]),
+            device_id_type=MESH,
+        )
+        scale = pltpu.make_async_remote_copy(
+            src_ref=scale_send.at[step - 1, i, h],
+            dst_ref=scale_recv.at[step - 1, i, h],
+            send_sem=scale_send_sem.at[step - 1, i, h],
+            recv_sem=scale_recv_sem.at[step - 1, i, h],
+            device_id=across(ORDERS[i][step - 1]),
+            device_id_type=MESH,
+        )
+        scale.start()
+        copy.start()
+        flying.extend((copy, scale))
+        return copy, scale
+
+    def encode(i, h, step, q, value):
+        top = jnp.max(jnp.abs(value), axis=0, keepdims=True)
+        steps = jnp.where(top > SMALLEST, LEVELS / jnp.maximum(top, SMALLEST), 0.0)
+        sends[step - 1][i, h, q] = jnp.round(value * steps).astype(jnp.int32).astype(WIRE)
+        scale_send[step - 1, i, h, pl.ds(q, 1)] = top * (1.0 / LEVELS)
+
+    def decode(i, h, step, q):
+        coded = recvs[step - 1][i, h, q].astype(jnp.int32).astype(jnp.float32)
+        return coded * scale_recv[step - 1, i, h, q : q + 1]
+
+    step_copies = {}
+
+    def multiply(i, part):
+        for pos in range(4 * part, 4 * part + 4):
+            acts_local[i, pos].wait()
+            acts_remote[i, pos].wait_recv()
+
+        @pl.loop(0, 4)
+        def _(q):
+            product = jnp.dot(cot_t[...], acts_buf[i, 4 * part + q], preferred_element_type=jnp.float32)
+            if part == 1:
+                for h in range(HALVES):
+                    encode(i, h, 1, q, product[h * half_width : (h + 1) * half_width])
+            else:
+                own[i, q] = product
+
+        if part == 1:
+            for h in range(HALVES):
+                step_copies[i, h, 1] = send_step(i, h, 1)
+
+    state_waited = []
+    one, two, share = scalars[0], scalars[1], scalars[2]
+
+    def finish(i, h, gradient_t):
+        if not state_waited:
+            for copy in state:
+                copy.wait()
+            state_waited.append(True)
+        lanes = slice(h * half_width, (h + 1) * half_width)
+        gradient = gradient_t.T / group_total
+        at = pl.ds(pl.multiple_of(column_piece(i) * cols, cols), cols)
+        weights = params[at, lanes]
+        fresh_first = beta_one * first[at, lanes] + (1.0 - beta_one) * gradient
+        fresh_second = beta_two * second[at, lanes] + (1.0 - beta_two) * gradient * gradient
+        ratio = fresh_first / one / (jnp.sqrt(fresh_second / two) + epsilon)
+        weighted = share * (weights - inner_rate * (ratio + decay_rate * weights))
+        if i < PIECES // 2:
+            weighted_send[i, h] = weighted
+            copy = pltpu.make_async_remote_copy(
+                src_ref=weighted_send.at[i, h],
+                dst_ref=weighted_recv.at[i, h],
+                send_sem=weighted_send_sem.at[i, h],
+                recv_sem=weighted_recv_sem.at[i, h],
+                device_id=peer,
+                device_id_type=MESH,
+            )
+            copy.start()
+            weighted_copies[i, h] = copy
+            return
+        n = i - PIECES // 2
+        weighted_copies[n, h].wait_recv()
+        mine = slice(n * cols, (n + 1) * cols)
+        new_anchor, new_momentum = outer_update(
+            anchor[mine, lanes], momentum[mine, lanes], weighted + weighted_recv[n, h]
+        )
+        rounded = new_anchor.astype(jnp.bfloat16)
+        fresh_send[n, h] = rounded
+        copy = pltpu.make_async_remote_copy(
+            src_ref=fresh_send.at[n, h],
+            dst_ref=fresh_recv.at[n, h],
+            send_sem=fresh_send_sem.at[n, h],
+            recv_sem=fresh_recv_sem.at[n, h],
+            device_id=peer,
+            device_id_type=MESH,
+        )
+        copy.start()
+        fresh_copies[n, h] = copy
+        anchor_out[mine, lanes] = new_anchor
+        momentum_out[mine, lanes] = new_momentum
+        at = pl.ds(pl.multiple_of(group * half_rows + n * cols, cols), cols)
+        weights_out[at, lanes] = rounded
+
+    weighted_copies = {}
+    fresh_copies = {}
+
+    def add(i, h, step):
+        for copy in step_copies[i, h, step]:
+            copy.wait_recv()
+        keys = slice(h * half_width, (h + 1) * half_width)
+        held = 8 >> step
+        if step == STEPS:
+            finish(i, h, own[i, 0, keys] + decode(i, h, step, 0))
+            return
+        keep = held // 2
+        for q in range(keep, held):
+            total = own[i, q, keys] + decode(i, h, step, q)
+            encode(i, h, step + 1, q - keep, total)
+        step_copies[i, h, step + 1] = send_step(i, h, step + 1)
+        for q in range(keep):
+            own[i, q, keys] += decode(i, h, step, q)
+
+    for event in PLAN:
+        if event[0] == "mul":
+            multiply(*event[1:])
+        else:
+            add(*event[1:])
+
+    for n in range(PIECES // 2):
+        for h in range(HALVES):
+            fresh_copies[n, h].wait_recv()
+            at = pl.ds(pl.multiple_of(other_group * half_rows + n * cols, cols), cols)
+            weights_out[at, h * half_width : (h + 1) * half_width] = fresh_recv[n, h]
+    cot_remote.wait_send()
+    for copy in list(acts_remote.values()) + flying + list(weighted_copies.values()) + list(fresh_copies.values()):
+        copy.wait_send()
+
+
+def fused_per_device(
+    acts, cotangent, inner_params, adam_first, adam_second, inner_steps, group_tokens, anchor, momentum
+):
+    group = lax.axis_index("group")
+    tokens, _ = acts.shape[1:]
+    rows, width = inner_params.shape[1:]
+    cols, half_width = rows // PIECES, width // HALVES
+    steps = lax.dynamic_index_in_dim(inner_steps, group, 0, False).astype(jnp.float32)
+    counts = group_tokens.astype(jnp.float32)
+    share = lax.dynamic_index_in_dim(counts, group, 0, False) / jnp.sum(counts)
+    scalars = jnp.stack(
+        [
+            1.0 - jnp.power(jnp.float32(beta_one), steps),
+            1.0 - jnp.power(jnp.float32(beta_two), steps),
+            share,
+        ]
+    )
+    low, full = jnp.bfloat16, jnp.float32
+    dma = pltpu.SemaphoreType.DMA
+    stage = [(PIECES, HALVES, 8 >> (s + 1), half_width, cols) for s in range(STEPS)]
+    tail = (PIECES // 2, HALVES, cols, half_width)
+    new_anchor, new_momentum, weights = pl.pallas_call(
+        functools.partial(outer_step_kernel, tokens * lax.axis_size("fsdp")),
+        out_shape=(
+            jax.ShapeDtypeStruct(anchor.shape, full),
+            jax.ShapeDtypeStruct(anchor.shape, full),
+            jax.ShapeDtypeStruct((rows, width), low),
+        ),
+        in_specs=[pl.BlockSpec(memory_space=pltpu.SMEM)] + [pl.BlockSpec(memory_space=pl.ANY)] * 7,
+        out_specs=[pl.BlockSpec(memory_space=pltpu.VMEM)] * 3,
+        scratch_shapes=[
+            pltpu.VMEM((PIECES, 8, 2 * tokens, cols), low),
+            pltpu.VMEM((2 * tokens, width), low),
+            pltpu.VMEM((width, 2 * tokens), low),
+            pltpu.VMEM((PIECES, 4, width, cols), full),
+            *[pltpu.VMEM(s, WIRE) for s in stage],
+            *[pltpu.VMEM(s, WIRE) for s in stage],
+            *[pltpu.VMEM((STEPS, PIECES, HALVES, 8, cols), full)] * 2,
+            *[pltpu.VMEM((rows, width), full)] * 3,
+            *[pltpu.VMEM((rows // 2, width), full)] * 2,
+            pltpu.VMEM(tail, full),
+            pltpu.VMEM(tail, full),
+            pltpu.VMEM(tail, low),
+            pltpu.VMEM(tail, low),
+            dma((PIECES, 8)),
+            dma((PIECES, 8)),
+            dma((PIECES, 8)),
+            dma((3,)),
+            dma((5,)),
+            *[dma((STEPS, PIECES, HALVES))] * 4,
+            dma((2, HALVES)),
+            dma((2, HALVES)),
+            dma((2, HALVES)),
+            dma((2, HALVES)),
+        ],
+        compiler_params=pltpu.CompilerParams(
+            collective_id=0, has_side_effects=True, vmem_limit_bytes=48 * 1024 * 1024
+        ),
+    )(scalars, acts[0], cotangent[0], inner_params[0], adam_first[0], adam_second[0], anchor, momentum)
+    return (new_anchor, new_momentum, weights[None])
+
+
+def choose(*arguments):
+    rows = arguments[2].shape[1]
+    fits = lax.axis_size("fsdp") == 1 << (STEPS + 1) and lax.axis_size("group") == 2
+    if fits and rows % (PIECES * 128) == 0 and arguments[2].shape[2] % (HALVES * 128) == 0:
+        return fused_per_device(*arguments)
+    return per_device(*arguments)
+
+
 def solution(mesh):
     placed = (
         P("group", "fsdp", None),
@@ -77,7 +443,7 @@
         P(("fsdp", "group"), None),
     )
     return jax.shard_map(
-        per_device,
+        choose,
         mesh=mesh,
         in_specs=placed,
         out_specs=(

time: 242 us -> 89.7 us (0.37)
  waiting for transfers between devices: 196 us -> 0 us
  Pallas kernels: 0 us -> 74.8 us
  between operations: 16.1 us -> 2.72 us
  matrix products: 11.7 us -> 0 us
  blocking collectives: 8.52 us -> 0 us
  local copies, waits for them, and re-layouts: 3.53 us -> 9.78 us
  other arithmetic: 6.32 us -> 2 us
    reduce_scatter x2 -> x0, waiting for transfers between devices: 196 us -> none  [the longest x1 176 us: per_device(): lax.psum_scatter(lax.dot_general(inputs, upstream, contract, preferred_el...]
    pallas_call x0 -> x1, Pallas kernels: none -> 74.8 us  [fused_per_device(): pl.pallas_call(functools.partial(outer_step_kernel, tokens * lax.axis_siz...]
    dot_general x1 -> x0, matrix products: 11.7 us -> none  [per_device(): lax.dot_general(inputs, upstream, contract, preferred_element_type=jnp.fl...]
    all_gather x1 -> x0, blocking collectives: 8.52 us -> none  [per_device(): lax.all_gather(new_anchor.astype(jnp.bfloat16), 'group', axis=0, tiled=True)]
    unnamed x13, local copies, waits for them, and re-layouts: 2.36 us -> 7.95 us
    mul x1 -> x0, other arithmetic: 3.36 us -> none  [per_device(): weighted = share * updated]
  transfers between devices with their start and end apart: 2 -> 0, of which waited for: 2 -> 0; matrix products, arithmetic and copies ran while one was open for 1% -> 0% of each run, Pallas kernels for 0% -> 0%
where the time goes in v1:
time: 89.7 us; the launch traced here: 89.3 us
  Pallas kernels  74.8 us (83%)
  local copies, waits for them, and re-layouts  9.78 us (11%)
  between operations  2.72 us (3%)
  other arithmetic  2 us (2%)
    pallas_call x1, Pallas kernels, fused_per_device(): pl.pallas_call(functools.partial(outer_step_kernel, tokens * lax.axis_siz...  74.8 us
    unnamed x13, local copies, waits for them, and re-layouts  7.95 us

profile of v1, /device:TPU:0, one launch (start us, length us, event | category | flops | bytes accessed | tf_op | source)
XLA Modules:
  0.0 89.3 jit_solution(3512903751238115596)
XLA Ops:
  0.6 1.3 %convert_reduce_fusion = f32[]{:T(128)} fusion(s32[2]{0:T(128)} %param.15), kind=kLoop, calls=%fused_computation.1 | loop fusion | flops 3 | bytes 12 | tf_op jit(solution)/shard_map/reduce_sum | solution.py:372
  1.9 1.2 %dynamic_slice.8 = s32[1]{0:T(128)} dynamic-slice(s32[2]{0:T(128)} %param.14, s32[]{:T(128)S(6)} %select_n.6), dynamic_slice_sizes={1} | dynamic-slice | bytes 12 | tf_op jit(solution)/shard_map/jit(dynamic_index_in_dim)/dynamic_slice | solution.py:370
  3.9 0.7 convert_element_type.8
  4.5 0.6 dynamic_slice.9
  6.5 0.1 pad_maximum_fusion.scalars
  6.5 0.0 copy-start
  6.5 1.2 %copy-done = f32[1,512,512]{2,1,0:T(8,128)S(1)} copy-done((f32[1,512,512]{2,1,0:T(8,128)S(1)}, f32[1,512,512]{2,1,0:T(8,128)}, u32[]{:S(2)}) %copy-start) | copy-done | bytes 1048600
  7.8 0.0 copy-start.1
  7.8 1.2 %copy-done.1 = f32[1,512,512]{2,1,0:T(8,128)S(1)} copy-done((f32[1,512,512]{2,1,0:T(8,128)S(1)}, f32[1,512,512]{2,1,0:T(8,128)}, u32[]{:S(2)}) %copy-start.1) | copy-done | bytes 1048600
  9.0 0.0 copy-start.2
  9.0 1.0 %copy-done.2 = bf16[1,512,512]{2,1,0:T(8,128)(2,1)S(1)} copy-done((bf16[1,512,512]{2,1,0:T(8,128)(2,1)S(1)}, bf16[1,512,512]{2,1,0:T(8,128)(2,1)}, u32[]{:S(2)}) %copy-start.2) | copy-done | bytes 524312
  10.0 0.0 copy-start.3
  10.0 1.0 %copy-done.3 = f32[256,512]{1,0:T(8,128)S(1)} copy-done((f32[256,512]{1,0:T(8,128)S(1)}, f32[256,512]{1,0:T(8,128)}, u32[]{:S(2)}) %copy-start.3) | copy-done | bytes 524312
  11.1 0.0 copy-start.4
  11.1 1.0 %copy-done.4 = f32[256,512]{1,0:T(8,128)S(1)} copy-done((f32[256,512]{1,0:T(8,128)S(1)}, f32[256,512]{1,0:T(8,128)}, u32[]{:S(2)}) %copy-start.4) | copy-done | bytes 524312
  12.1 74.8 %shard_map.112 = (f32[256,512]{1,0:T(8,128)S(1)}, f32[256,512]{1,0:T(8,128)S(1)}, bf16[512,512]{1,0:T(8,128)(2,1)S(1)}) custom-call(f32[3]{0:T(128)S(1)} %pad_maximum_fusion.scalars, bf16[512,8192]{1,0:T(8,128)(2,1)} %bitcast.12, bf16[512,512]{1,0:T(8,128)(2,1)S(1)} %bitcast.10, f32[512,512]{1,0:T(8,128)S(1)} %bitcast.8, f32[512,512]{1,0:T(8,128)S(1)} %bitcast.9, ...), custom_call_target="tpu_custom_call" | custom-call | tf_op jit(solution)/shard_map/pallas_call | solution.py:384
  86.9 0.8 copy.15
  87.7 0.8 copy.16
  88.5 0.8 copy.17
Async XLA Ops:
  6.5 1.2 %copy-start = (f32[1,512,512]{2,1,0:T(8,128)S(1)}, f32[1,512,512]{2,1,0:T(8,128)}, u32[]{:S(2)}) copy-start(f32[1,512,512]{2,1,0:T(8,128)} %param.11) | copy-start | bytes 3145732
  7.8 1.2 %copy-start.1 = (f32[1,512,512]{2,1,0:T(8,128)S(1)}, f32[1,512,512]{2,1,0:T(8,128)}, u32[]{:S(2)}) copy-start(f32[1,512,512]{2,1,0:T(8,128)} %param.12) | copy-start | bytes 3145732
  9.0 1.0 %copy-start.2 = (bf16[1,512,512]{2,1,0:T(8,128)(2,1)S(1)}, bf16[1,512,512]{2,1,0:T(8,128)(2,1)}, u32[]{:S(2)}) copy-start(bf16[1,512,512]{2,1,0:T(8,128)(2,1)} %param.10) | copy-start | bytes 1572868
  10.0 1.0 %copy-start.3 = (f32[256,512]{1,0:T(8,128)S(1)}, f32[256,512]{1,0:T(8,128)}, u32[]{:S(2)}) copy-start(f32[256,512]{1,0:T(8,128)} %anchor_in.1) | copy-start | bytes 1572868
  11.1 1.0 %copy-start.4 = (f32[256,512]{1,0:T(8,128)S(1)}, f32[256,512]{1,0:T(8,128)}, u32[]{:S(2)}) copy-start(f32[256,512]{1,0:T(8,128)} %momentum_in.1) | copy-start | bytes 1572868
